TPU v7x, 32 devices: a whole 2x2x4 slice. The times are simulated.
32 devices in a mesh: dp: 8 (over y, x, core), mp: 4 (over z).
Axes of the slice: x: 2, y: 2, z: 4, core: 2. Of those that a mesh axis runs over, the one named last changes fastest.
Arguments:
- tokens: bfloat16 [5120, 768], P('dp'), may hold values from -6 to 6
- segment_ids: int32 [8, 640], P('dp'), may hold values from 0 to 3, never falling along the last dimension, each value on 1 to 320 neighbouring positions
- token_types: int32 [8, 640], P('dp'), may hold values 0 or 1
- q_weight: bfloat16 [4, 768, 768], P(None, None, 'mp'), may hold values from -0.21875 to 0.21875
- k_weight: bfloat16 [768, 768], P(None, 'mp'), may hold values from -0.21875 to 0.21875
- v_weight: bfloat16 [768, 768], P(None, 'mp'), may hold values from -0.21875 to 0.21875
- o_weight: bfloat16 [768, 768], P('mp'), may hold values from -2.5 to 2.5
- o_bias: float32 [768], replicated, may hold values from -1.5 to 1.5
- norm1_gain: float32 [768], replicated, may hold values from 0.25 to 1.75
- norm1_shift: float32 [768], replicated, may hold values from -1.5 to 1.5
- in_weight: bfloat16 [768, 3072], P(None, 'mp'), may hold values from -0.21875 to 0.21875
- in_bias: float32 [3072], P('mp'), may hold values from -1.5 to 1.5
- out_weight: bfloat16 [3072, 768], P('mp'), may hold values from -0.109375 to 0.109375
- out_bias: float32 [768], replicated, may hold values from -1.5 to 1.5
- norm2_gain: float32 [768], replicated, may hold values from 0.25 to 1.75
- norm2_shift: float32 [768], replicated, may hold values from -1.5 to 1.5
- cotangent: bfloat16 [5120, 768], P('dp'), may hold values from -6 to 6
Outputs:
- layer_out: bfloat16 [5120, 768], P('dp')
- tokens_grad: bfloat16 [5120, 768], P('dp')
- q_grad: float32 [4, 768, 768], P(None, 'dp', 'mp')
- k_grad: float32 [768, 768], P('dp', 'mp')
- v_grad: float32 [768, 768], P('dp', 'mp')
- o_grad: float32 [768, 768], P('mp', 'dp')
- o_bias_grad: float32 [768], replicated
- norm1_gain_grad: float32 [768], replicated
- norm1_shift_grad: float32 [768], replicated
- in_grad: float32 [768, 3072], P('dp', 'mp')
- in_bias_grad: float32 [3072], P('mp')
- out_grad: float32 [3072, 768], P('mp', 'dp')
- out_bias_grad: float32 [768], replicated
- norm2_gain_grad: float32 [768], replicated
- norm2_shift_grad: float32 [768], replicated
Inputs may be any that keep to these rules, and one draw needn't show every extreme that they name: `segment_ids`: a sequence's rows with equal ids form one run.
All inputs are finite; a program needn't handle non-finite values. No bound on the sum of `token_types` on one device may be relied on, other than what follows from the above.
Results may differ from a plain program's by a relative error of at most 0.019.
Values may be sent and summed in bfloat16 or wider, within the bound.
A program may use at most 128 MiB of HBM per device.

v0:
```python
import jax
import jax.numpy as jnp
from jax import lax
from jax.sharding import PartitionSpec as P

HD = 64
norm_epsilon = 1e-05


def layer_norm(inputs, gain, shift):
    average = jnp.mean(inputs, axis=-1, keepdims=True)
    centred = inputs - average
    spread = jnp.mean(centred * centred, axis=-1, keepdims=True)
    return centred * lax.rsqrt(spread + norm_epsilon) * gain + shift


def gelu_exact(inputs):
    return jax.nn.gelu(inputs, approximate=False)


def matmul(left, right):
    return jnp.dot(left, right, preferred_element_type=jnp.float32)


def local(
    tokens,
    segment_ids,
    token_types,
    q_weight,
    k_weight,
    v_weight,
    o_weight,
    o_bias,
    norm1_gain,
    norm1_shift,
    in_weight,
    in_bias,
    out_weight,
    out_bias,
    norm2_gain,
    norm2_shift,
    cotangent,
):
    row_count = tokens.shape[0]
    groups, length = segment_ids.shape
    local_width = k_weight.shape[1]
    head_count = local_width // HD
    score_scale = HD ** (-0.5)
    entity = token_types == 1
    chooser = entity[:, :, None, None]
    key_entity = entity[:, None, None, :]
    same_doc = (segment_ids[:, :, None] == segment_ids[:, None, :])[:, None]
    share_rows = row_count // lax.axis_size("mp")
    row_offset = lax.axis_index("mp") * share_rows
    queries = jnp.einsum(
        "rd,tdc->trc", tokens, q_weight, preferred_element_type=jnp.float32
    ).astype(jnp.bfloat16)
    keys = matmul(tokens, k_weight).astype(jnp.bfloat16)
    values = matmul(tokens, v_weight).astype(jnp.bfloat16)
    query_four = queries.reshape(4, groups, length, head_count, HD)
    query_word = jnp.where(chooser, query_four[2], query_four[0])
    query_ent = jnp.where(chooser, query_four[3], query_four[1])
    key_heads = keys.reshape(groups, length, head_count, HD)
    value_heads = values.reshape(groups, length, head_count, HD)

    def scores_now():
        raw_word = jnp.einsum(
            "gqhc,gkhc->ghqk", query_word, key_heads, preferred_element_type=jnp.float32
        )
        raw_ent = jnp.einsum(
            "gqhc,gkhc->ghqk", query_ent, key_heads, preferred_element_type=jnp.float32
        )
        raw_all = jnp.where(key_entity, raw_ent, raw_word)
        return jnp.where(same_doc, raw_all * score_scale, -1000000000.0)

    scores = scores_now()
    highest = jnp.max(scores, axis=-1, keepdims=True)
    log_total = highest + jnp.log(jnp.sum(jnp.exp(scores - highest), axis=-1, keepdims=True))
    attention_low = jnp.exp(scores - log_total).astype(jnp.bfloat16)
    mixed = jnp.einsum(
        "ghqk,gkhc->gqhc", attention_low, value_heads, preferred_element_type=jnp.float32
    )
    mixed = mixed.reshape(row_count, local_width).astype(jnp.bfloat16)
    token_wide = tokens.astype(jnp.float32)
    branch = lax.psum(matmul(mixed, o_weight), "mp") + o_bias
    hidden, norm1_pull = jax.vjp(layer_norm, token_wide + branch, norm1_gain, norm1_shift)
    hidden_low = hidden.astype(jnp.bfloat16)
    inner_pre = matmul(hidden_low, in_weight) + in_bias
    activated, gelu_pull = jax.vjp(gelu_exact, inner_pre)
    activated_low = activated.astype(jnp.bfloat16)
    ffn_out = (
        lax.psum(matmul(activated_low, out_weight).astype(jnp.bfloat16), "mp").astype(jnp.float32)
        + out_bias
    )
    result, norm2_pull = jax.vjp(layer_norm, hidden + ffn_out, norm2_gain, norm2_shift)
    layer_out = result.astype(jnp.bfloat16)
    d_res2, d_gain2, d_shift2 = norm2_pull(cotangent.astype(jnp.float32))
    d_out_bias = jnp.sum(d_res2, axis=0)
    grad_ffn = d_res2.astype(jnp.bfloat16)
    d_out_weight = matmul(activated_low.T, grad_ffn)
    (d_inner,) = gelu_pull(matmul(grad_ffn, out_weight.T))
    d_in_bias = jnp.sum(d_inner, axis=0)
    inner_low = d_inner.astype(jnp.bfloat16)
    d_in_weight = matmul(hidden_low.T, inner_low)
    d_hidden = d_res2 + lax.psum(matmul(inner_low, in_weight.T).astype(jnp.bfloat16), "mp").astype(
        jnp.float32
    )
    d_res1, d_gain1, d_shift1 = norm1_pull(d_hidden)
    d_o_bias = jnp.sum(d_res1, axis=0)
    grad_branch = d_res1.astype(jnp.bfloat16)
    d_o_weight = matmul(mixed.T, grad_branch)
    d_mixed = matmul(grad_branch, o_weight.T).astype(jnp.bfloat16)
    mixed_heads = d_mixed.reshape(groups, length, head_count, HD)
    attention = jnp.exp(scores_now() - log_total)
    d_probs = jnp.einsum(
        "gqhc,gkhc->ghqk", mixed_heads, value_heads, preferred_element_type=jnp.float32
    )
    d_values = jnp.einsum(
        "ghqk,gqhc->gkhc",
        attention.astype(jnp.bfloat16),
        mixed_heads,
        preferred_element_type=jnp.float32,
    )
    row_delta = jnp.sum(attention * d_probs, axis=-1, keepdims=True)
    d_raw = (attention * (d_probs - row_delta) * score_scale).astype(jnp.bfloat16)
    nothing = jnp.zeros_like(d_raw)
    raw_word = jnp.where(key_entity, nothing, d_raw)
    raw_ent = jnp.where(key_entity, d_raw, nothing)
    d_query_word = jnp.einsum(
        "ghqk,gkhc->gqhc", raw_word, key_heads, preferred_element_type=jnp.float32
    )
    d_query_ent = jnp.einsum(
        "ghqk,gkhc->gqhc", raw_ent, key_heads, preferred_element_type=jnp.float32
    )
    d_keys = jnp.einsum(
        "ghqk,gqhc->gkhc", raw_word, query_word, preferred_element_type=jnp.float32
    ) + jnp.einsum("ghqk,gqhc->gkhc", raw_ent, query_ent, preferred_element_type=jnp.float32)
    empty_rows = jnp.zeros_like(d_query_word)
    d_queries = (
        jnp.stack(
            [
                jnp.where(chooser, empty_rows, d_query_word),
                jnp.where(chooser, empty_rows, d_query_ent),
                jnp.where(chooser, d_query_word, empty_rows),
                jnp.where(chooser, d_query_ent, empty_rows),
            ]
        )
        .reshape(4, row_count, local_width)
        .astype(jnp.bfloat16)
    )
    d_keys_low = d_keys.reshape(row_count, local_width).astype(jnp.bfloat16)
    d_values_low = d_values.reshape(row_count, local_width).astype(jnp.bfloat16)
    d_q_weight = jnp.einsum("rd,trc->tdc", tokens, d_queries, preferred_element_type=jnp.float32)
    d_k_weight = matmul(tokens.T, d_keys_low)
    d_v_weight = matmul(tokens.T, d_values_low)
    res_rows = lax.dynamic_slice_in_dim(d_res1, row_offset, share_rows, 0)
    total = jnp.einsum("trc,tdc->rd", d_queries, q_weight, preferred_element_type=jnp.float32)
    grad_rows = (
        res_rows
        + lax.psum_scatter(
            (total + matmul(d_keys_low, k_weight.T) + matmul(d_values_low, v_weight.T)).astype(
                jnp.bfloat16
            ),
            "mp",
            scatter_dimension=0,
            tiled=True,
        ).astype(jnp.float32)
    ).astype(jnp.bfloat16)
    tokens_grad = lax.all_gather(grad_rows, "mp", axis=0, tiled=True)
    d_q_weight, d_k_weight, d_v_weight, d_o_weight, d_in_weight, d_out_weight = (
        lax.psum_scatter(d_q_weight, "dp", scatter_dimension=1, tiled=True),
        lax.psum_scatter(d_k_weight, "dp", scatter_dimension=0, tiled=True),
        lax.psum_scatter(d_v_weight, "dp", scatter_dimension=0, tiled=True),
        lax.psum_scatter(d_o_weight, "dp", scatter_dimension=1, tiled=True),
        lax.psum_scatter(d_in_weight, "dp", scatter_dimension=0, tiled=True),
        lax.psum_scatter(d_out_weight, "dp", scatter_dimension=1, tiled=True),
    )
    d_o_bias, d_gain1, d_shift1, d_in_bias, d_out_bias, d_gain2, d_shift2 = lax.psum(
        (d_o_bias, d_gain1, d_shift1, d_in_bias, d_out_bias, d_gain2, d_shift2), "dp"
    )
    return (
        layer_out,
        tokens_grad,
        d_q_weight,
        d_k_weight,
        d_v_weight,
        d_o_weight,
        d_o_bias,
        d_gain1,
        d_shift1,
        d_in_weight,
        d_in_bias,
        d_out_weight,
        d_out_bias,
        d_gain2,
        d_shift2,
    )


def solution(mesh):
    return jax.shard_map(
        local,
        mesh=mesh,
        in_specs=(
            P("dp", None),
            P("dp", None),
            P("dp", None),
            P(None, None, "mp"),
            P(None, "mp"),
            P(None, "mp"),
            P("mp", None),
            P(),
            P(),
            P(),
            P(None, "mp"),
            P("mp"),
            P("mp", None),
            P(),
            P(),
            P(),
            P("dp", None),
        ),
        out_specs=(
            P("dp", None),
            P("dp", None),
            P(None, "dp", "mp"),
            P("dp", "mp"),
            P("dp", "mp"),
            P("mp", "dp"),
            P(),
            P(),
            P(),
            P("dp", "mp"),
            P("mp"),
            P("mp", "dp"),
            P(),
            P(),
            P(),
        ),
        check_vma=False,
    )
```

profile of v0, /device:TPU:0, one launch (start us, length us, event | category | flops | bytes accessed | tf_op | source)
XLA Modules:
  0.0 547.0 jit_solution(5020968630286662695)
XLA Ops:
  22.2 84.7 %all-reduce.5.cloned.1.call-done = f32[640,768]{1,0:T(8,128)} async-done(((f32[640,768]{1,0:T(8,128)}), f32[640,768]{1,0:T(8,128)}) %all-reduce.5.cloned.1.call-update) | async-done | bytes 1966096 | tf_op jit(solution)/shard_map/psum | solution.py:85
  109.7 6.5 %multiply_convert_fusion.1 = (bf16[640,768]{1,0:T(8,128)(2,1)S(1)}, f32[640,768]{1,0:T(8,128)}, f32[640,768]{1,0:T(8,128)}) fusion(f32[768]{0:T(1024)S(1)} %copy-done.36, bf16[768,768]{1,0:T(8,128)(2,1)S(1)} %copy-done, f32[640,768]{1,0:T(8,128)S(1)} %get-tuple-element.70, f32[768]{0:T(1024)S(1)} %copy-done.31, f32[768]{0:T(1024)S(1)} %copy-done.27, ...), kind=kOutput, calls=%fused_computation.32 | convolution fusion | flops 789872640 | bytes 8075264 | tf_op jit(solution)/shard_map/dot_general | solution.py:22
  119.6 48.5 %all-reduce.7.cloned.1.call-done = bf16[640,768]{1,0:T(8,128)(2,1)} async-done(((bf16[640,768]{1,0:T(8,128)(2,1)}), bf16[640,768]{1,0:T(8,128)(2,1)}) %all-reduce.7.cloned.1.call-update) | async-done | bytes 983056 | tf_op jit(solution)/shard_map/psum | solution.py:92
  179.6 49.1 %all-reduce.9.cloned.1.call-done = bf16[640,768]{1,0:T(8,128)(2,1)} async-done(((bf16[640,768]{1,0:T(8,128)(2,1)}), bf16[640,768]{1,0:T(8,128)(2,1)}) %all-reduce.9.cloned.1.call-update) | async-done | bytes 983056 | tf_op jit(solution)/shard_map/psum | solution.py:105
  228.7 3.1 multiply_reduce_fusion.1
  235.9 3.4 convolution_convert_fusion.3
  239.3 3.1 fusion.82
  242.4 9.7 %fusion.21 = f32[3,64,640]{2,1,0:T(8,128)} fusion(pred[640]{0:T(1024)(128)(4,1)S(1)} %compare_reduce_fusion, f32[3,640,640]{1,2,0:T(8,128)} %fusion.82, f32[3,640,640]{1,2,0:T(8,128)} %copy-done.2, f32[3,640]{1,0:T(4,128)S(1)} %log_add_fusion, bf16[640,3,64]{0,2,1:T(8,128)(2,1)S(1)} %bitcast.122, bf16[640,3,64]{0,2,1:T(8,128)(2,1)S(1)} %bitcast.120), kind=kOutput, calls=%fused_computation.69 | convolution fusion | flops 167242240 | bytes 10821760 | tf_op jit(solution)/shard_map/ghqk,gqhc->gkhc/dot_general | solution.py:135
  252.1 9.6 %convolution_bitcast_fusion.4 = bf16[1,3,64,640]{3,2,1,0:T(8,128)(2,1)} fusion(bf16[640,3,64]{0,2,1:T(8,128)(2,1)S(1)} %bitcast.104, pred[640]{0:T(1024)(128)(4,1)S(1)} %compare_reduce_fusion, f32[3,640,640]{1,2,0:T(8,128)} %fusion.82, f32[3,640,640]{1,2,0:T(8,128)} %copy-done.2, f32[3,640]{1,0:T(4,128)S(1)} %log_add_fusion), kind=kOutput, calls=%fused_computation.60 | convolution fusion | flops 167119360 | bytes 10330240 | tf_op jit(solution)/shard_map/ghqk,gkhc->gqhc/dot_general | solution.py:132
  263.7 9.3 %fusion.20 = bf16[3,64,640]{2,1,0:T(8,128)(2,1)S(1)} fusion(f32[3,64,640]{2,1,0:T(8,128)} %fusion.21, pred[640]{0:T(1024)(128)(4,1)S(1)} %compare_reduce_fusion, f32[3,640,640]{1,2,0:T(8,128)} %fusion.82, f32[3,640,640]{1,2,0:T(8,128)} %copy-done.2, f32[3,640]{1,0:T(4,128)S(1)} %log_add_fusion, bf16[640,3,64]{0,2,1:T(8,128)(2,1)} %bitcast.118, ...), kind=kOutput, calls=%fused_computation.63 | convolution fusion | flops 167488000 | bytes 11067520 | tf_op jit(solution)/shard_map/ghqk,gqhc->gkhc/dot_general | solution.py:137
  272.9 9.9 %select_convert_fusion.3 = (bf16[1,3,64,640]{3,2,1,0:T(8,128)(2,1)}, bf16[1,3,64,640]{3,2,1,0:T(8,128)(2,1)}, bf16[1,3,64,640]{3,2,1,0:T(8,128)(2,1)}, bf16[1,3,64,640]{3,2,1,0:T(8,128)(2,1)}) fusion(pred[640]{0:T(1024)(128)(4,1)S(1)} %compare_reduce_fusion, bf16[1,3,64,640]{3,2,1,0:T(8,128)(2,1)} %convolution_bitcast_fusion.4, ...), kind=kOutput, calls=%fused_computation.79 | convolution fusion | flops 167610880 | bytes 11313280 | tf_op jit(solution)/shard_map/ghqk,gkhc->gqhc/dot_general | solution.py:129
  284.5 3.6 fusion.12
  288.2 3.9 convolution_bitcast_fusion
  292.1 4.5 copy.56
  296.6 4.7 reshape.292
  309.6 4.2 fusion.64
  315.0 2.8 fusion.44
  317.8 24.7 %all-reduce = (f32[768]{0:T(1024)}, f32[768]{0:T(1024)}, f32[768]{0:T(1024)}, f32[768]{0:T(1024)}, f32[768]{0:T(1024)}, /*index=5*/f32[768]{0:T(1024)}, f32[768]{0:T(1024)}) all-reduce(f32[768]{0:T(1024)S(1)} %get-tuple-element.59, f32[768]{0:T(1024)S(1)} %get-tuple-element.45, ...), channel_id=1, replica_groups=mesh['dp'=8,'mp'=4] {'dp'}, use_global_device_ids=true, to_apply=%region_20.21 | all-reduce | flops 5376 | bytes 43008 | tf_op jit(solution)/shard_map/psum | solution.py:178
  345.3 19.9 %all_gather.3 = bf16[640,768]{1,0:T(8,128)(2,1)S(1)} all-gather(bf16[160,768]{1,0:T(8,128)(2,1)S(1)} %add_convert_fusion.2), channel_id=1, replica_groups=mesh['dp'=8,'mp'=4] {'mp'}, dimensions={0}, use_global_device_ids=true | all-gather | bytes 1228800 | tf_op jit(solution)/shard_map/all_gather | solution.py:169
  365.2 3.9 reduce-scatter.22.cloned.1.call-done
  371.2 36.6 %reduce-scatter.26.cloned.1.call-done = f32[96,192]{1,0:T(8,128)} async-done(((f32[768,192]{1,0:T(8,128)}), f32[96,192]{1,0:T(8,128)}) %reduce-scatter.26.cloned.1.call-update) | async-done | bytes 73744
  407.8 38.7 %reduce-scatter.24.cloned.1.call-done = f32[96,192]{1,0:T(8,128)} async-done(((f32[768,192]{1,0:T(8,128)}), f32[96,192]{1,0:T(8,128)}) %reduce-scatter.24.cloned.1.call-update) | async-done | bytes 73744
  446.5 46.3 %reduce-scatter.20.cloned.1.call-done = f32[768,96]{0,1:T(8,128)} async-done(((f32[768,768]{0,1:T(8,128)}), f32[768,96]{0,1:T(8,128)}) %reduce-scatter.20.cloned.1.call-update) | async-done | bytes 294928 | tf_op jit(solution)/shard_map/reduce_scatter | solution.py:176
  492.8 46.1 %reduce-scatter.18.cloned.1.call-done = f32[96,768]{1,0:T(8,128)} async-done(((f32[768,768]{1,0:T(8,128)}), f32[96,768]{1,0:T(8,128)}) %reduce-scatter.18.cloned.1.call-update) | async-done | bytes 294928 | tf_op jit(solution)/shard_map/reduce_scatter | solution.py:175
  (157 shorter events, 55.3 us)
Async XLA Ops:
  7.2 102.2 %copy-start = (bf16[768,768]{1,0:T(8,128)(2,1)S(1)}, bf16[768,768]{1,0:T(8,128)(2,1)}, u32[]{:S(2)}) copy-start(bf16[768,768]{1,0:T(8,128)(2,1)} %param.27) | copy-start | bytes 3538948
  7.2 4.8 copy-start.3
  7.2 4.5 copy-start.33
  7.2 99.6 %all-reduce.5.cloned.1.call-start = ((), (), s32[]{:S(2)}) async-start(), calls=%async_computation.7 | async-start | bytes 3932160 | tf_op jit(solution)/shard_map/psum | solution.py:85
  9.8 5.6 %copy-start.10 = (bf16[640,192]{0,1:T(8,128)(2,1)}, bf16[640,192]{0,1:T(8,128)(2,1)S(1)}, u32[]{:S(2)}) copy-start(bf16[640,192]{0,1:T(8,128)(2,1)S(1)} %convolution_convert_fusion.6) | copy-start | bytes 737284
  11.7 6.1 %copy-start.12 = (bf16[640,192]{0,1:T(8,128)(2,1)}, bf16[640,192]{0,1:T(8,128)(2,1)S(1)}, u32[]{:S(2)}) copy-start(bf16[640,192]{0,1:T(8,128)(2,1)S(1)} %convolution_convert_fusion.7) | copy-start | bytes 737284
  20.3 86.6 %copy-start.29 = (f32[768]{0:T(1024)S(1)}, f32[768]{0:T(1024)}, u32[]{:S(2)}) copy-start(f32[768]{0:T(1024)} %param.24) | copy-start | bytes 9220
  22.1 146.0 %all-reduce.7.cloned.1.call-start = ((), (), s32[]{:S(2)}) async-start(), calls=%async_computation.8 | async-start | bytes 1966080 | tf_op jit(solution)/shard_map/psum | solution.py:92
  109.7 7.5 %copy-start.34 = (bf16[768,768]{1,0:T(8,128)(2,1)S(1)}, bf16[768,768]{1,0:T(8,128)(2,1)}, u32[]{:S(2)}) copy-start(bf16[768,768]{1,0:T(8,128)(2,1)} %param.29) | copy-start | bytes 3538948
  117.2 50.9 %copy-start.30 = (f32[768]{0:T(1024)S(1)}, f32[768]{0:T(1024)}, u32[]{:S(2)}) copy-start(f32[768]{0:T(1024)} %param.30) | copy-start | bytes 9220
  119.1 109.6 %all-reduce.9.cloned.1.call-start = ((), (), s32[]{:S(2)}) async-start(), calls=%async_computation.9 | async-start | bytes 1966080 | tf_op jit(solution)/shard_map/psum | solution.py:105
  179.5 163.0 %reduce-scatter.28.cloned.1.call-start = ((), (), s32[]{:S(2)}) async-start(), calls=%async_computation.16 | async-start | bytes 884736
  242.4 9.7 %copy-start.11 = (bf16[640,192]{0,1:T(8,128)(2,1)S(1)}, bf16[640,192]{0,1:T(8,128)(2,1)}, u32[]{:S(2)}) copy-start(bf16[640,192]{0,1:T(8,128)(2,1)} %copy-done.10) | copy-start | bytes 737284
  252.1 9.8 %copy-start.17 = (bf16[768,192]{0,1:T(8,128)(2,1)S(1)}, bf16[768,192]{0,1:T(8,128)(2,1)}, u32[]{:S(2)}) copy-start(bf16[768,192]{0,1:T(8,128)(2,1)} %param.22) | copy-start | bytes 884740
  261.7 82.4 %reduce-scatter.16.cloned.1.call-start = ((), (), s32[]{:S(2)}) async-start(), calls=%async_computation.10 | async-start | bytes 1228800 | tf_op jit(solution)/shard_map/reduce_scatter | solution.py:160
  272.9 9.9 %copy-start.19 = (bf16[3,64,640]{2,1,0:T(8,128)(2,1)}, bf16[3,64,640]{2,1,0:T(8,128)(2,1)S(1)}, u32[]{:S(2)}) copy-start(bf16[3,64,640]{2,1,0:T(8,128)(2,1)S(1)} %fusion.20) | copy-start | bytes 737284
  272.9 9.9 %copy-start.18 = (bf16[768,192]{0,1:T(8,128)(2,1)S(1)}, bf16[768,192]{0,1:T(8,128)(2,1)}, u32[]{:S(2)}) copy-start(bf16[768,192]{0,1:T(8,128)(2,1)} %param.21) | copy-start | bytes 884740
  284.5 3.7 copy-start.4
  288.1 81.0 %reduce-scatter.22.cloned.1.call-start = ((), (), s32[]{:S(2)}) async-start(), calls=%async_computation.13 | async-start | bytes 2654208
  301.3 106.5 %reduce-scatter.26.cloned.1.call-start = ((), (), s32[]{:S(2)}) async-start(), calls=%async_computation.15 | async-start | bytes 884736
  304.8 141.7 %reduce-scatter.24.cloned.1.call-start = ((), (), s32[]{:S(2)}) async-start(), calls=%async_computation.14 | async-start | bytes 884736
  309.5 183.3 %reduce-scatter.20.cloned.1.call-start = ((), (), s32[]{:S(2)}) async-start(), calls=%async_computation.12 | async-start | bytes 2654208 | tf_op jit(solution)/shard_map/reduce_scatter | solution.py:176
  313.8 225.2 %reduce-scatter.18.cloned.1.call-start = ((), (), s32[]{:S(2)}) async-start(), calls=%async_computation.11 | async-start | bytes 2654208 | tf_op jit(solution)/shard_map/reduce_scatter | solution.py:175
  345.3 194.6 %copy-start.1 = (bf16[768,768]{1,0:T(8,128)(2,1)S(1)}, bf16[768,768]{1,0:T(8,128)(2,1)}, u32[]{:S(2)}) copy-start(bf16[768,768]{1,0:T(8,128)(2,1)} %param.27) | copy-start | bytes 3538948
  (31 other events, 52.7 us)
Sparse Core Ops, SparseCore 0:
  22.2 84.5 all-reduce.4
  119.2 48.8 all-reduce.6
  179.6 49.0 all-reduce.8
  261.8 34.1 reduce-scatter.27
  298.7 26.2 reduce-scatter.15
  328.2 40.9 reduce-scatter.21
  372.9 34.9 reduce-scatter.25
  411.6 34.9 reduce-scatter.23
  450.5 42.3 reduce-scatter.19
  496.6 42.3 reduce-scatter.17
where the time goes:
time: 554 us; the launch traced here: 547 us
  waiting for transfers between devices  354 us (64%)
  matrix products  90 us (16%)
  blocking collectives  44.6 us (8%)
  local copies, waits for them, and re-layouts  27.3 us (5%)
  between operations  14.9 us (3%)
  other arithmetic  14.8 us (3%)
    psum x1, waiting for transfers between devices, local(): branch = lax.psum(matmul(mixed, o_weight), 'mp') + o_bias  84.7 us
    unnamed x14, waiting for transfers between devices  79.4 us
    psum x1, waiting for transfers between devices, local(): lax.psum(matmul(inner_low, in_weight.T).astype(jnp.bfloat16), 'mp')  49.1 us
    psum x1, waiting for transfers between devices, local(): lax.psum(matmul(activated_low, out_weight).astype(jnp.bfloat16), 'mp')  48.5 us
    reduce_scatter x1, waiting for transfers between devices, local(): lax.psum_scatter(d_out_weight, 'dp', scatter_dimension=1, tiled=True)  46.3 us
    reduce_scatter x1, waiting for transfers between devices, local(): lax.psum_scatter(d_in_weight, 'dp', scatter_dimension=0, tiled=True)  46.1 us
    dot_general x14, matrix products, matmul(): return jnp.dot(left, right, preferred_element_type=jnp.float32)  30.4 us
    unnamed x98, local copies, waits for them, and re-layouts  27.2 us
  transfers between devices with their start and end apart: 10, of which 8 were waited for; matrix products, arithmetic and copies ran while one was open for 11% of the time, Pallas kernels for 0%

commit v1 on v0

--- a/solution.py
+++ b/solution.py
@@ -166,7 +166,14 @@
             tiled=True,
         ).astype(jnp.float32)
     ).astype(jnp.bfloat16)
-    tokens_grad = lax.all_gather(grad_rows, "mp", axis=0, tiled=True)
+    ways, here, hop = (lax.axis_size("mp"), lax.axis_index("mp"), grad_rows.shape[0])
+    line, have = (grad_rows, 1)
+    while have < ways:
+        line = jnp.concatenate(
+            [line, lax.ppermute(line, "mp", [(d, (d - have) % ways) for d in range(ways)])], axis=0
+        )
+        have = 2 * have
+    tokens_grad = jnp.roll(line, here * hop, axis=0)
     d_q_weight, d_k_weight, d_v_weight, d_o_weight, d_in_weight, d_out_weight = (
         lax.psum_scatter(d_q_weight, "dp", scatter_dimension=1, tiled=True),
         lax.psum_scatter(d_k_weight, "dp", scatter_dimension=0, tiled=True),

time: 554 us -> 579 us (1.045)
  waiting for transfers between devices: 354 us -> 377 us
  blocking collectives: 44.6 us -> 23.7 us
  starting transfers between devices: 1.26 us -> 14.9 us
  local copies, waits for them, and re-layouts: 27.3 us -> 33.4 us
    unnamed x14, waiting for transfers between devices: 79.4 us -> 108 us
    all_gather x1 -> x0, blocking collectives: 19.9 us -> none  [local(): tokens_grad = lax.all_gather(grad_rows, 'mp', axis=0, tiled=True)]
    psum x1, waiting for transfers between devices: 48.5 us -> 37.2 us  [local(): lax.psum(matmul(activated_low, out_weight).astype(jnp.bfloat16), 'mp')]
    psum x1, starting transfers between devices: 0.51 us -> 11.8 us  [local(): lax.psum(matmul(inner_low, in_weight.T).astype(jnp.bfloat16), 'mp')]
    ppermute x0 -> x2, waiting for transfers between devices: none -> 6.16 us  [local(): lax.ppermute(line, 'mp', [(d, (d - have) % ways) for d in range(ways)])]
    unnamed x98 -> x103, local copies, waits for them, and re-layouts: 27.2 us -> 30 us
  transfers between devices with their start and end apart: 10 -> 12, of which waited for: 8 -> 9; matrix products, arithmetic and copies ran while one was open for 11% -> 8% of each run, Pallas kernels for 0% -> 0%
where the time goes in v1:
time: 579 us; the launch traced here: 571 us
  waiting for transfers between devices  377 us (65%)
  matrix products  88.9 us (15%)
  local copies, waits for them, and re-layouts  33.4 us (6%)
  blocking collectives  23.7 us (4%)
  other arithmetic  17.5 us (3%)
  between operations  15.1 us (3%)
  starting transfers between devices  14.9 us (3%)
    unnamed x14, waiting for transfers between devices  108 us
    psum x1, waiting for transfers between devices, local(): branch = lax.psum(matmul(mixed, o_weight), 'mp') + o_bias  84.7 us
    psum x1, waiting for transfers between devices, local(): lax.psum(matmul(inner_low, in_weight.T).astype(jnp.bfloat16), 'mp')  49.1 us
    reduce_scatter x1, waiting for transfers between devices, local(): lax.psum_scatter(d_out_weight, 'dp', scatter_dimension=1, tiled=True)  46.3 us
    reduce_scatter x1, waiting for transfers between devices, local(): lax.psum_scatter(d_in_weight, 'dp', scatter_dimension=0, tiled=True)  46.1 us
    psum x1, waiting for transfers between devices, local(): lax.psum(matmul(activated_low, out_weight).astype(jnp.bfloat16), 'mp')  37.2 us
    dot_general x14, matrix products, matmul(): return jnp.dot(left, right, preferred_element_type=jnp.float32)  30.3 us
    unnamed x103, local copies, waits for them, and re-layouts  30 us
  transfers between devices with their start and end apart: 12, of which 9 were waited for; matrix products, arithmetic and copies ran while one was open for 8% of the time, Pallas kernels for 0%

profile of v1, /device:TPU:0, one launch (start us, length us, event | category | flops | bytes accessed | tf_op | source)
XLA Modules:
  0.0 571.0 jit_solution(15752521169432833405)
XLA Ops:
  22.2 84.7 %all-reduce.5.cloned.1.call-done = f32[640,768]{1,0:T(8,128)} async-done(((f32[640,768]{1,0:T(8,128)}), f32[640,768]{1,0:T(8,128)}) %all-reduce.5.cloned.1.call-update) | async-done | bytes 1966096 | tf_op jit(solution)/shard_map/psum | solution.py:85
  109.7 6.5 %multiply_convert_fusion.1 = (bf16[640,768]{1,0:T(8,128)(2,1)S(1)}, f32[640,768]{1,0:T(8,128)}, f32[640,768]{1,0:T(8,128)}) fusion(f32[768]{0:T(1024)S(1)} %copy-done.34, bf16[768,768]{1,0:T(8,128)(2,1)S(1)} %copy-done, f32[640,768]{1,0:T(8,128)S(1)} %get-tuple-element.72, f32[768]{0:T(1024)S(1)} %copy-done.29, f32[768]{0:T(1024)S(1)} %copy-done.25, ...), kind=kOutput, calls=%fused_computation.32 | convolution fusion | flops 789872640 | bytes 8075264 | tf_op jit(solution)/shard_map/dot_general | solution.py:22
  119.1 11.8 %all-reduce.9.cloned.1.call-start = ((), (), s32[]{:S(2)}) async-start(), calls=%async_computation.9 | async-start | bytes 1966080 | tf_op jit(solution)/shard_map/psum | solution.py:105
  130.9 37.2 %all-reduce.7.cloned.1.call-done = bf16[640,768]{1,0:T(8,128)(2,1)} async-done(((bf16[640,768]{1,0:T(8,128)(2,1)}), bf16[640,768]{1,0:T(8,128)(2,1)}) %all-reduce.7.cloned.1.call-update) | async-done | bytes 983056 | tf_op jit(solution)/shard_map/psum | solution.py:92
  179.6 49.1 %all-reduce.9.cloned.1.call-done = bf16[640,768]{1,0:T(8,128)(2,1)} async-done(((bf16[640,768]{1,0:T(8,128)(2,1)}), bf16[640,768]{1,0:T(8,128)(2,1)}) %all-reduce.9.cloned.1.call-update) | async-done | bytes 983056 | tf_op jit(solution)/shard_map/psum | solution.py:105
  228.7 3.1 multiply_reduce_fusion.1
  237.8 3.1 fusion.82
  240.9 9.7 %fusion.21 = f32[3,64,640]{2,1,0:T(8,128)} fusion(pred[640]{0:T(1024)(128)(4,1)S(1)} %compare_reduce_fusion, f32[3,640,640]{1,2,0:T(8,128)} %fusion.82, f32[3,640,640]{1,2,0:T(8,128)} %copy-done.2, f32[3,640]{1,0:T(4,128)S(1)} %log_add_fusion, bf16[640,3,64]{0,2,1:T(8,128)(2,1)S(1)} %bitcast.124, bf16[640,3,64]{0,2,1:T(8,128)(2,1)S(1)} %bitcast.122), kind=kOutput, calls=%fused_computation.69 | convolution fusion | flops 167242240 | bytes 10821760 | tf_op jit(solution)/shard_map/ghqk,gqhc->gkhc/dot_general | solution.py:135
  250.6 9.6 %convolution_bitcast_fusion.4 = bf16[1,3,64,640]{3,2,1,0:T(8,128)(2,1)} fusion(bf16[640,3,64]{0,2,1:T(8,128)(2,1)S(1)} %bitcast.106, pred[640]{0:T(1024)(128)(4,1)S(1)} %compare_reduce_fusion, f32[3,640,640]{1,2,0:T(8,128)} %fusion.82, f32[3,640,640]{1,2,0:T(8,128)} %copy-done.2, f32[3,640]{1,0:T(4,128)S(1)} %log_add_fusion), kind=kOutput, calls=%fused_computation.60 | convolution fusion | flops 167119360 | bytes 10330240 | tf_op jit(solution)/shard_map/ghqk,gkhc->gqhc/dot_general | solution.py:132
  261.9 9.1 %fusion.20 = bf16[3,64,640]{2,1,0:T(8,128)(2,1)S(1)} fusion(f32[3,64,640]{2,1,0:T(8,128)} %fusion.21, pred[640]{0:T(1024)(128)(4,1)S(1)} %compare_reduce_fusion, f32[3,640,640]{1,2,0:T(8,128)} %fusion.82, f32[3,640,640]{1,2,0:T(8,128)} %copy-done.2, f32[3,640]{1,0:T(4,128)S(1)} %log_add_fusion, bf16[640,3,64]{0,2,1:T(8,128)(2,1)} %bitcast.120, ...), kind=kOutput, calls=%fused_computation.63 | convolution fusion | flops 167488000 | bytes 11067520 | tf_op jit(solution)/shard_map/ghqk,gqhc->gkhc/dot_general | solution.py:137
  271.0 10.0 %select_convert_fusion.3 = (bf16[1,3,64,640]{3,2,1,0:T(8,128)(2,1)S(1)}, bf16[1,3,64,640]{3,2,1,0:T(8,128)(2,1)}, bf16[1,3,64,640]{3,2,1,0:T(8,128)(2,1)}, bf16[1,3,64,640]{3,2,1,0:T(8,128)(2,1)}) fusion(pred[640]{0:T(1024)(128)(4,1)S(1)} %compare_reduce_fusion, bf16[1,3,64,640]{3,2,1,0:T(8,128)(2,1)} %convolution_bitcast_fusion.4, ...), kind=kOutput, calls=%fused_computation.80 | convolution fusion | flops 167610880 | bytes 11313280 | tf_op jit(solution)/shard_map/ghqk,gkhc->gqhc/dot_general | solution.py:129
  282.7 3.4 fusion.12
  286.3 3.2 convolution_bitcast_fusion.1
  289.5 3.9 convolution_bitcast_fusion
  293.4 4.5 copy.56
  297.9 4.7 reshape.292
  310.8 4.2 fusion.64
  322.6 6.2 %collective-permute-done = bf16[160,768]{1,0:T(8,128)(2,1)S(1)} collective-permute-done((bf16[160,768]{1,0:T(8,128)(2,1)S(1)}, bf16[160,768]{1,0:T(8,128)(2,1)S(1)}, u32[]{:S(2)}, u32[]{:S(2)}) %collective-permute-start) | collective-permute-done | bytes 245792 | tf_op jit(solution)/shard_map/ppermute | solution.py:173
  330.0 23.7 %all-reduce = (f32[768]{0:T(1024)}, f32[768]{0:T(1024)}, f32[768]{0:T(1024)}, f32[768]{0:T(1024)}, f32[768]{0:T(1024)}, /*index=5*/f32[768]{0:T(1024)}, f32[768]{0:T(1024)}) all-reduce(f32[768]{0:T(1024)S(1)} %get-tuple-element.59, f32[768]{0:T(1024)S(1)} %get-tuple-element.45, ...), channel_id=1, replica_groups=mesh['dp'=8,'mp'=4] {'dp'}, use_global_device_ids=true, to_apply=%region_20.21 | all-reduce | flops 5376 | bytes 43008 | tf_op jit(solution)/shard_map/psum | solution.py:185
  361.6 32.4 %reduce-scatter.22.cloned.1.call-done = f32[96,768]{1,0:T(8,128)} async-done(((f32[768,768]{1,0:T(8,128)}), f32[96,768]{1,0:T(8,128)}) %reduce-scatter.22.cloned.1.call-update) | async-done | bytes 294928
  396.1 36.6 %reduce-scatter.26.cloned.1.call-done = f32[96,192]{1,0:T(8,128)} async-done(((f32[768,192]{1,0:T(8,128)}), f32[96,192]{1,0:T(8,128)}) %reduce-scatter.26.cloned.1.call-update) | async-done | bytes 73744
  432.7 38.7 %reduce-scatter.24.cloned.1.call-done = f32[96,192]{1,0:T(8,128)} async-done(((f32[768,192]{1,0:T(8,128)}), f32[96,192]{1,0:T(8,128)}) %reduce-scatter.24.cloned.1.call-update) | async-done | bytes 73744
  471.4 46.3 %reduce-scatter.20.cloned.1.call-done = f32[768,96]{0,1:T(8,128)} async-done(((f32[768,768]{0,1:T(8,128)}), f32[768,96]{0,1:T(8,128)}) %reduce-scatter.20.cloned.1.call-update) | async-done | bytes 294928 | tf_op jit(solution)/shard_map/reduce_scatter | solution.py:183
  517.7 46.1 %reduce-scatter.18.cloned.1.call-done = f32[96,768]{1,0:T(8,128)} async-done(((f32[768,768]{1,0:T(8,128)}), f32[96,768]{1,0:T(8,128)}) %reduce-scatter.18.cloned.1.call-update) | async-done | bytes 294928 | tf_op jit(solution)/shard_map/reduce_scatter | solution.py:182
  (169 shorter events, 68.1 us)
Async XLA Ops:
  7.2 102.2 %copy-start = (bf16[768,768]{1,0:T(8,128)(2,1)S(1)}, bf16[768,768]{1,0:T(8,128)(2,1)}, u32[]{:S(2)}) copy-start(bf16[768,768]{1,0:T(8,128)(2,1)} %param.27) | copy-start | bytes 3538948
  7.2 99.6 %all-reduce.5.cloned.1.call-start = ((), (), s32[]{:S(2)}) async-start(), calls=%async_computation.7 | async-start | bytes 3932160 | tf_op jit(solution)/shard_map/psum | solution.py:85
  9.8 5.6 copy-start.8
  11.7 6.1 %copy-start.11 = (bf16[640,192]{0,1:T(8,128)(2,1)}, bf16[640,192]{0,1:T(8,128)(2,1)S(1)}, u32[]{:S(2)}) copy-start(bf16[640,192]{0,1:T(8,128)(2,1)S(1)} %convolution_convert_fusion.7) | copy-start | bytes 737284
  20.3 86.6 %copy-start.27 = (f32[768]{0:T(1024)S(1)}, f32[768]{0:T(1024)}, u32[]{:S(2)}) copy-start(f32[768]{0:T(1024)} %param.24) | copy-start | bytes 9220
  22.1 146.0 %all-reduce.7.cloned.1.call-start = ((), (), s32[]{:S(2)}) async-start(), calls=%async_computation.8 | async-start | bytes 1966080 | tf_op jit(solution)/shard_map/psum | solution.py:92
  109.7 7.5 %copy-start.32 = (bf16[768,768]{1,0:T(8,128)(2,1)S(1)}, bf16[768,768]{1,0:T(8,128)(2,1)}, u32[]{:S(2)}) copy-start(bf16[768,768]{1,0:T(8,128)(2,1)} %param.29) | copy-start | bytes 3538948
  117.2 50.9 %copy-start.28 = (f32[768]{0:T(1024)S(1)}, f32[768]{0:T(1024)}, u32[]{:S(2)}) copy-start(f32[768]{0:T(1024)} %param.30) | copy-start | bytes 9220
  119.1 109.6 %all-reduce.9.cloned.1.call-start = ((), (), s32[]{:S(2)}) async-start(), calls=%async_computation.9 | async-start | bytes 1966080 | tf_op jit(solution)/shard_map/psum | solution.py:105
  179.5 139.6 %reduce-scatter.16.cloned.1.call-start = ((), (), s32[]{:S(2)}) async-start(), calls=%async_computation.10 | async-start | bytes 1228800 | tf_op jit(solution)/shard_map/reduce_scatter | solution.py:160
  228.7 8.1 %slice-start = ((s8[4915200]{0:T(1024)(128)(4,1)}), s8[4194304]{0:T(1024)(128)(4,1)S(1)}, s32[]{:S(2)}) async-start(s8[4915200]{0:T(1024)(128)(4,1)} %bitcast.99), calls=%async_computation.17 | async-start | bytes 8388608
  240.9 9.7 %copy-start.9 = (bf16[640,192]{0,1:T(8,128)(2,1)S(1)}, bf16[640,192]{0,1:T(8,128)(2,1)}, u32[]{:S(2)}) copy-start(bf16[640,192]{0,1:T(8,128)(2,1)} %copy-done.8) | copy-start | bytes 737284
  250.6 9.6 %copy-start.15 = (bf16[768,192]{0,1:T(8,128)(2,1)S(1)}, bf16[768,192]{0,1:T(8,128)(2,1)}, u32[]{:S(2)}) copy-start(bf16[768,192]{0,1:T(8,128)(2,1)} %param.22) | copy-start | bytes 884740
  271.0 10.0 %copy-start.17 = (bf16[3,64,640]{2,1,0:T(8,128)(2,1)}, bf16[3,64,640]{2,1,0:T(8,128)(2,1)S(1)}, u32[]{:S(2)}) copy-start(bf16[3,64,640]{2,1,0:T(8,128)(2,1)S(1)} %fusion.20) | copy-start | bytes 737284
  271.0 10.0 %copy-start.16 = (bf16[768,192]{0,1:T(8,128)(2,1)S(1)}, bf16[768,192]{0,1:T(8,128)(2,1)}, u32[]{:S(2)}) copy-start(bf16[768,192]{0,1:T(8,128)(2,1)} %param.21) | copy-start | bytes 884740
  286.2 67.5 %reduce-scatter.28.cloned.1.call-start = ((), (), s32[]{:S(2)}) async-start(), calls=%async_computation.16 | async-start | bytes 884736
  289.5 104.5 %reduce-scatter.22.cloned.1.call-start = ((), (), s32[]{:S(2)}) async-start(), calls=%async_computation.13 | async-start | bytes 2654208
  302.7 130.0 %reduce-scatter.26.cloned.1.call-start = ((), (), s32[]{:S(2)}) async-start(), calls=%async_computation.15 | async-start | bytes 884736
  306.2 165.1 %reduce-scatter.24.cloned.1.call-start = ((), (), s32[]{:S(2)}) async-start(), calls=%async_computation.14 | async-start | bytes 884736
  310.8 206.9 %reduce-scatter.20.cloned.1.call-start = ((), (), s32[]{:S(2)}) async-start(), calls=%async_computation.12 | async-start | bytes 2654208 | tf_op jit(solution)/shard_map/reduce_scatter | solution.py:183
  315.1 248.7 %reduce-scatter.18.cloned.1.call-start = ((), (), s32[]{:S(2)}) async-start(), calls=%async_computation.11 | async-start | bytes 2654208 | tf_op jit(solution)/shard_map/reduce_scatter | solution.py:182
  321.0 7.8 %collective-permute-start = (bf16[160,768]{1,0:T(8,128)(2,1)S(1)}, bf16[160,768]{1,0:T(8,128)(2,1)S(1)}, u32[]{:S(2)}, u32[]{:S(2)}) collective-permute-start(bf16[160,768]{1,0:T(8,128)(2,1)S(1)} %get-tuple-element.62), channel_id=1, source_target_pairs={{0,3},{1,0},{2,1},{3,2},{4,7},{5,4},{6,5},{7,6},{8,11},{9,8},{10,9... | collective-permute-start | bytes 737288 | tf_op jit(solution)/shard_map/ppermute | solution.py:173
  328.8 27.2 %collective-permute-start.1 = (bf16[320,768]{1,0:T(8,128)(2,1)S(1)}, bf16[320,768]{1,0:T(8,128)(2,1)S(1)}, u32[]{:S(2)}, u32[]{:S(2)}) collective-permute-start(bf16[320,768]{1,0:T(8,128)(2,1)S(1)} %pad_maximum_fusion.1), channel_id=1, source_target_pairs={{0,2},{1,3},{2,0},{3,1},{4,6},{5,7},{6,4},{7,5},{8,10},{9,11},{10,... | collective-permute-start | bytes 1474568 | tf_op jit(solution)/shard_map/ppermute | solution.py:173
  358.4 205.4 %copy-start.1 = (bf16[768,768]{1,0:T(8,128)(2,1)S(1)}, bf16[768,768]{1,0:T(8,128)(2,1)}, u32[]{:S(2)}) copy-start(bf16[768,768]{1,0:T(8,128)(2,1)} %param.27) | copy-start | bytes 3538948
  (34 other events, 67.9 us)
Sparse Core Ops, SparseCore 0:
  22.2 84.5 all-reduce.4
  119.2 48.8 all-reduce.6
  179.6 49.0 all-reduce.8
  286.3 25.4 reduce-scatter.15
  314.8 33.5 reduce-scatter.27
  351.6 42.3 reduce-scatter.21
  397.7 34.9 reduce-scatter.25
  436.4 34.9 reduce-scatter.23
  475.3 42.3 reduce-scatter.19
  521.4 42.3 reduce-scatter.17
